TPU v7x, 256 devices: a whole 4x4x8 slice. The times are simulated.
256 devices in a mesh: shard: 32 (over y, x, core), dp: 8 (over z).
Axes of the slice: x: 4, y: 4, z: 8, core: 2. Of those that a mesh axis runs over, the one named last changes fastest.
Arguments:
- grad: float32 [288, 128, 4096], P('shard', 'dp'), may hold values from -252 to 252
- param: bfloat16 [288, 128, 4096], P('shard', 'dp'), may hold values from -0.119628906 to 0.119628906
- row_state: float32 [288, 128], P('shard', 'dp'), may hold values from 0.3 to 27
- col_state: float32 [3, 4096], replicated, may hold values from 0.002 to 400
- block_start: int32 [32], replicated, may hold values from 0 to 143, as said below
- block_matrix: int32 [144], replicated, may hold values from 0 to 2, as said below
- step: int32 [1], replicated, may hold values from 2 to 11
Outputs:
- new_params: bfloat16 [18432, 4096], P(None, 'shard')
- new_row_state: float32 [288, 128], P('shard', 'dp')
- new_col_state: float32 [3, 4096], replicated
Inputs may be any that keep to these rules, and one draw needn't show every extreme that they name: block_start rises from 0 at index 0; every shard index owns between 1 and 9 consecutive global blocks, held in its first slots, and some index owns exactly 9; slots past a device's owned count hold values that no output reads. `block_matrix`: ids 0 and 1 each label 4096 / 128 blocks and id 2 labels 10240 / 128 blocks, in any order.
All inputs are finite; a program needn't handle non-finite values.
Results may differ from a plain program's by a relative error of at most 0.0004.
Values may be sent and summed in bfloat16 or wider, within the bound.
A program may use at most 64 MiB of HBM per device.

v0:
```python
import jax
import jax.numpy as jnp
from jax import lax
from jax.sharding import Mesh
from jax.sharding import PartitionSpec as P

D = 4096
FF = 10240
SHARD = ("shard_0", "shard_1", "shard_2")


def cut_along(shard, dim, length):
    shape = shard.shape
    blocks = shard.reshape(*shape[:dim], length, shape[dim] // length, *shape[dim + 1 :])
    return jnp.moveaxis(blocks, dim, 0)


def summed_on_arrival(shard, axis, dim):
    length = lax.axis_size(axis)
    blocks = lax.all_to_all(cut_along(shard, dim, length), axis, 0, 0, tiled=True)
    return jnp.sum(blocks, axis=0)


def summed_rows(shard, axes, dim):
    far, near = axes
    blocks = cut_along(shard, dim, lax.axis_size(far))
    nearer = summed_on_arrival(blocks, near, dim + 1)
    arrived = lax.all_to_all(nearer, far, split_axis=0, concat_axis=0, tiled=True)
    return arrived.sum(axis=0)


def filled_up(lines, length):
    spare = -lines.shape[0] % length
    if not spare:
        return lines
    return jnp.concatenate([lines, jnp.zeros((spare, *lines.shape[1:]), lines.dtype)])


def sent_to_all(shard, axis):
    copies = jnp.broadcast_to(shard, (lax.axis_size(axis), *shard.shape))
    return lax.all_to_all(copies, axis, split_axis=0, concat_axis=0, tiled=True)


def in_order(blocks, dim):
    shape = list(blocks.shape[1:])
    shape[dim] *= blocks.shape[0]
    return jnp.moveaxis(blocks, 0, dim).reshape(shape)


def whole_of(shard, axes, dim):
    far, near = axes
    blocks = sent_to_all(sent_to_all(shard, far), near)
    return in_order(blocks.swapaxes(0, 1).reshape(-1, *shard.shape), dim)


def sum_by_parts(shard, axes):
    own = summed_rows(filled_up(shard, lax.axis_size(axes[0]) * lax.axis_size(axes[1])), axes, 0)
    whole = whole_of(own, axes, 0)
    return whole[: len(shard)].reshape(shard.shape)


def together(arrays, axis):
    ravelled, at, gathered = (jnp.concatenate([a.reshape(-1) for a in arrays]), 0, [])
    subtotal = sum_by_parts(ravelled, axis)
    for a in arrays:
        gathered.append(subtotal[at : at + a.size].reshape(a.shape))
        at += a.size
    return tuple(gathered)


def moved_by_axis(blocks, axes, turns):
    shape = [lax.axis_size(a) for a in axes]
    blocks = blocks.reshape(*shape, *blocks.shape[1:])
    for k in turns:
        blocks = lax.all_to_all(blocks, axes[k], split_axis=k, concat_axis=k, tiled=True)
    return blocks.reshape(-1, *blocks.shape[len(axes) :])


def exchange_by_chip(shard, groups, turns, split_dim, concat_dim):
    length = lax.axis_size(groups[0]) * lax.axis_size(groups[1])
    blocks = cut_along(shard, split_dim, length)
    return in_order(moved_by_axis(blocks, groups, turns), concat_dim)


def scale_grad(grad, safe_rows, matrix_pick, new_cols, row_avg):
    slot_cols = jnp.dot(matrix_pick, new_cols, precision=lax.Precision.HIGHEST)
    slot_avg = jnp.dot(matrix_pick, row_avg, precision=lax.Precision.HIGHEST)
    return grad / jnp.sqrt(safe_rows[:, :, None] * slot_cols[:, None, :] / slot_avg[:, None, None])


def body(grad, param, row_state, col_state, block_start, block_matrix, step):
    slot_count = grad.shape[0]
    total_blocks = block_matrix.shape[0]
    shard_index = lax.axis_index(SHARD)
    block_ends = jnp.concatenate([block_start[1:], jnp.full((1,), total_blocks, jnp.int32)])
    first_block = lax.dynamic_index_in_dim(block_start, shard_index, keepdims=False)
    owned_count = lax.dynamic_index_in_dim(block_ends, shard_index, keepdims=False) - first_block
    slot_ids = jnp.arange(slot_count, dtype=jnp.int32)
    live_slot = slot_ids < owned_count
    block_ids = first_block + slot_ids
    block_table = block_ids[:, None] == jnp.arange(total_blocks, dtype=jnp.int32)[None, :]
    matrix_ids = jnp.sum(jnp.where(block_table, block_matrix[None, :], 0), axis=1)
    matrix_ids = jnp.where(live_slot, matrix_ids, 0)
    matrix_pick = (matrix_ids[:, None] == jnp.arange(3, dtype=jnp.int32)[None, :]).astype(
        jnp.float32
    )
    member = matrix_pick * live_slot[:, None].astype(jnp.float32)
    row_count = jnp.array([D, D, FF], jnp.float32)
    step_value = step[0].astype(jnp.float32)
    decay_rate = 1.0 - step_value ** (-0.8)
    learn_rate = 1.0 / jnp.sqrt(jnp.maximum(step_value, 10000.0))
    squares = grad * grad
    new_rows = jnp.where(
        live_slot[:, None],
        decay_rate * row_state + (1.0 - decay_rate) * jnp.sum(squares, axis=2) / D,
        0.0,
    )
    safe_rows = jnp.where(live_slot[:, None], new_rows, 1.0)
    col_part = jnp.einsum(
        "sm,sd->md", member, jnp.sum(squares, axis=1), precision=lax.Precision.HIGHEST
    )
    row_part = jnp.dot(jnp.sum(new_rows, axis=1), member, precision=lax.Precision.HIGHEST)
    quot_part = jnp.einsum(
        "sm,sd->md",
        member,
        jnp.sum(squares / safe_rows[:, :, None], axis=1),
        precision=lax.Precision.HIGHEST,
    )
    col_total, quot_total, row_total = together(
        (col_part, quot_part, row_part), (("shard_0", "shard_1"), ("shard_2", "dp"))
    )
    new_cols = decay_rate * col_state + (1.0 - decay_rate) * col_total / row_count[:, None]
    row_avg = row_total / row_count
    scaled = scale_grad(grad, safe_rows, matrix_pick, new_cols, row_avg)
    square_total = row_avg * jnp.sum(quot_total / new_cols, axis=1)
    clip_factor = jnp.maximum(1.0, jnp.sqrt(square_total / (row_count * D)))
    slot_clip = jnp.dot(matrix_pick, clip_factor, precision=lax.Precision.HIGHEST)
    updated = jnp.where(
        live_slot[:, None, None],
        param.astype(jnp.float32) - learn_rate * scaled / slot_clip[:, None, None],
        0.0,
    ).astype(jnp.bfloat16)
    column_rows = exchange_by_chip(updated, (("shard_0", "shard_1"), "shard_2"), (1, 0), 2, 0)
    spread = lax.all_gather(column_rows, "dp", axis=1, tiled=True)
    block_index = jnp.arange(total_blocks, dtype=jnp.int32)
    block_owner = (
        jnp.sum((block_start[None, :] <= block_index[:, None]).astype(jnp.int32), axis=1) - 1
    )
    slot_of = block_owner * slot_count + block_index - jnp.take(block_start, block_owner)
    new_params = jnp.take(spread, slot_of, axis=0).reshape(
        total_blocks * spread.shape[1], spread.shape[2]
    )
    return (new_params, new_rows, new_cols)


def solution(mesh):
    finer = Mesh(
        mesh.devices.reshape(4, 4, 2, mesh.shape["dp"]), ("shard_0", "shard_1", "shard_2", "dp")
    )
    in_specs = (P(SHARD, "dp", None), P(SHARD, "dp", None), P(SHARD, "dp"), P(), P(), P(), P())
    out_specs = (P(None, SHARD), P(SHARD, "dp"), P())
    return jax.shard_map(body, mesh=finer, in_specs=in_specs, out_specs=out_specs, check_vma=False)
```

profile of v0, /device:TPU:2, one launch (start us, length us, event | category | flops | bytes accessed | tf_op | source)
XLA Modules:
  0.0 263.2 jit_solution(12649364172545486583)
XLA Ops:
  13.1 1.9 multiply_reduce_fusion.1
  16.5 1.6 divide_reduce_fusion
  20.1 1.5 reshape.144
  21.5 2.0 fusion.3
  23.5 1.5 reshape.143
  26.4 1.5 concatenate.7
  27.9 1.8 reshape_reshape.9
  30.7 17.0 %all_to_all.38 = f32[16,16,97]{2,1,0:T(8,128)} all-to-all(f32[16,16,97]{2,1,0:T(8,128)S(1)} %copy.23), channel_id=1, replica_groups=mesh['shard_0'=4,'shard_1'=4,'shard_2'=2,'dp'=8] {'shard_2','dp'}, dimensions={0} | all-to-all | bytes 198656 | tf_op jit(solution)/shard_map/all_to_all | solution.py:20
  48.6 13.6 %all_to_all.39 = f32[16,1,97]{2,1,0:T(1,128)} all-to-all(f32[16,1,97]{2,1,0:T(1,128)S(1)} %bitcast.48), channel_id=1, replica_groups=mesh['shard_0'=4,'shard_1'=4,'shard_2'=2,'dp'=8] {'shard_0','shard_1'}, dimensions={0} | all-to-all | bytes 12416 | tf_op jit(solution)/shard_map/all_to_all | solution.py:28
  63.0 10.6 %all_to_all.40 = f32[16,1,97]{2,1,0:T(1,128)S(1)} all-to-all(f32[16,1,97]{2,1,0:T(1,128)S(1)} %broadcast_in_dim.106), channel_id=1, replica_groups=mesh['shard_0'=4,'shard_1'=4,'shard_2'=2,'dp'=8] {'shard_0','shard_1'}, dimensions={0} | all-to-all | bytes 12416 | tf_op jit(solution)/shard_map/all_to_all | solution.py:41
  74.2 4.2 %all-to-all-start.3 = ((f32[16,16,97]{2,1,0:T(8,128)}), f32[16,16,97]{2,1,0:T(8,128)}, u32[]{:S(2)}, u32[]{:S(2)}) async-start(f32[16,16,97]{2,1,0:T(8,128)} %broadcast_in_dim.107), calls=%async_computation.3 | async-start | bytes 262144 | tf_op jit(solution)/shard_map/all_to_all | solution.py:41
  78.5 8.4 %all-to-all-done.3 = f32[16,16,97]{2,1,0:T(8,128)} async-done(((f32[16,16,97]{2,1,0:T(8,128)}), f32[16,16,97]{2,1,0:T(8,128)}, u32[]{:S(2)}, u32[]{:S(2)}) %all-to-all-start.3) | async-done | bytes 99360 | tf_op jit(solution)/shard_map/all_to_all | solution.py:41
  86.8 1.6 copy.24
  88.4 1.7 reshape_reshape.10
  90.2 1.5 slice_multiply_fusion
  91.6 1.4 mul.105
  93.1 1.4 reshape.145
  98.5 1.6 select_convert_fusion
  100.8 4.7 %all_to_all.41 = bf16[16,2,9,16,128]{4,3,2,0,1:T(8,128)(2,1)S(1)} all-to-all(bf16[16,2,9,16,128]{4,3,2,0,1:T(8,128)(2,1)S(1)} %copy.26), channel_id=1, replica_groups=mesh['shard_0'=4,'shard_1'=4,'shard_2'=2,'dp'=8] {'shard_2'}, dimensions={1} | all-to-all | bytes 2359296 | tf_op jit(solution)/shard_map/all_to_all | solution.py:75
  105.7 22.5 %all_to_all.42 = bf16[16,2,9,16,128]{4,3,2,1,0:T(8,128)(2,1)} all-to-all(bf16[16,2,9,16,128]{4,3,2,1,0:T(8,128)(2,1)S(1)} %copy.27), channel_id=1, replica_groups=mesh['shard_0'=4,'shard_1'=4,'shard_2'=2,'dp'=8] {'shard_0','shard_1'}, dimensions={0} | all-to-all | bytes 2359296 | tf_op jit(solution)/shard_map/all_to_all | solution.py:75
  128.4 1.6 gather_fusion
  130.1 101.9 %all-gather.2.cloned.1.call-done = bf16[288,128,128]{2,1,0:T(8,128)(2,1)} async-done(((bf16[288,16,128]{2,1,0:T(8,128)(2,1)}), bf16[288,128,128]{2,1,0:T(8,128)(2,1)}) %all-gather.2.cloned.1.call-update) | async-done | bytes 9437200 | tf_op jit(solution)/shard_map/all_gather | solution.py:144
  232.0 11.3 %gather_fusion.1 = bf16[144,128,128]{2,1,0:T(8,128)(2,1)} fusion(bf16[288,128,128]{2,1,0:T(8,128)(2,1)} %all-gather.2.cloned.1.call-done, s32[1024]{0:T(1024)S(1)} %pad_clamp_fusion), kind=kCustom, calls=%fused_computation.1 | custom fusion | bytes 9437760 | tf_op jit(solution)/shard_map/jit(_take)/gather | solution.py:150
  243.3 13.0 %bitcast_select_fusion = bf16[18432,128]{1,0:T(8,128)(2,1)} fusion(bf16[144,128,128]{2,1,0:T(8,128)(2,1)} %gather_fusion.1, pred[18432]{0:T(1024)(128)(4,1)S(1)} %broadcast_bitcast_fusion), kind=kLoop, calls=%fused_computation.2 | loop fusion | flops 2359296 | bytes 9455616 | tf_op jit(solution)/shard_map/jit(_take)/select_n | solution.py:150
  (53 shorter events, 17.1 us)
Async XLA Ops:
  7.2 9.3 %copy-start.1 = (f32[9,16,4096]{2,1,0:T(8,128)S(1)}, f32[9,16,4096]{2,1,0:T(8,128)}, u32[]{:S(2)}) copy-start(f32[9,16,4096]{2,1,0:T(8,128)} %param.8) | copy-start | bytes 7077892
  7.2 7.9 %copy-start.5 = (f32[9,16]{1,0:T(8,128)S(1)}, f32[9,16]{1,0:T(8,128)}, u32[]{:S(2)}) copy-start(f32[9,16]{1,0:T(8,128)} %param.10) | copy-start | bytes 1732
  12.4 3.5 %copy-start.7 = (pred[9]{0:T(512)(128)(4,1)}, pred[9]{0:T(512)(128)(4,1)S(1)}, u32[]{:S(2)}) copy-start(pred[9]{0:T(512)(128)(4,1)S(1)} %get-tuple-element.13) | copy-start | bytes 31
  13.1 5.0 %copy-start.8 = (s32[144]{0:T(256)S(1)}, s32[144]{0:T(256)}, u32[]{:S(2)}) copy-start(s32[144]{0:T(256)} %param.13) | copy-start | bytes 1732
  15.9 0.6 copy-start.4
  18.1 80.4 %copy-start.2 = (bf16[9,16,4096]{2,1,0:T(8,128)(2,1)S(1)}, bf16[9,16,4096]{2,1,0:T(8,128)(2,1)}, u32[]{:S(2)}) copy-start(bf16[9,16,4096]{2,1,0:T(8,128)(2,1)} %param.9) | copy-start | bytes 3538948
  19.0 11.6 %copy-start.6 = (s32[9]{0:T(128)}, s32[9]{0:T(128)S(1)}, u32[]{:S(2)}) copy-start(s32[9]{0:T(128)S(1)} %broadcast_select_fusion.1) | copy-start | bytes 112
  74.2 12.7 %all-to-all-start.3 = ((f32[16,16,97]{2,1,0:T(8,128)}), f32[16,16,97]{2,1,0:T(8,128)}, u32[]{:S(2)}, u32[]{:S(2)}) async-start(f32[16,16,97]{2,1,0:T(8,128)} %broadcast_in_dim.107), calls=%async_computation.3 | async-start | bytes 262144 | tf_op jit(solution)/shard_map/all_to_all | solution.py:41
  78.4 153.6 %all-gather.2.cloned.1.call-start = ((), (), s32[]{:S(2)}) async-start(), calls=%async_computation.6 | async-start | bytes 10616832 | tf_op jit(solution)/shard_map/all_gather | solution.py:144
  96.6 1.9 copy-start.3
  105.7 22.5 %copy-start = (s32[32]{0:T(128)S(1)}, s32[32]{0:T(128)}, u32[]{:S(2)}) copy-start(s32[32]{0:T(128)} %param.12) | copy-start | bytes 388
Sparse Core Ops, SparseCore 0:
  128.4 103.5 all-gather.1
where the time goes:
time: 265 us; the launch traced here: 263 us
  waiting for transfers between devices  110 us (42%)
  blocking collectives  68.3 us (26%)
  local copies, waits for them, and re-layouts  31.3 us (12%)
  other arithmetic  25.5 us (10%)
  between operations  16.3 us (6%)
  matrix products  7.16 us (3%)
  starting transfers between devices  4.21 us (2%)
    all_gather x1, waiting for transfers between devices, body(): spread = lax.all_gather(column_rows, 'dp', axis=1, tiled=True)  102 us
    all_to_all x2, blocking collectives, moved_by_axis(): lax.all_to_all(blocks, axes[k], split_axis=k, concat_axis=k, tiled=True)  27.2 us
    all_to_all x1, blocking collectives, summed_on_arrival(): lax.all_to_all(cut_along(shard, dim, length), axis, 0, 0, tiled=True)  17 us
    all_to_all x1, blocking collectives, summed_rows(): lax.all_to_all(nearer, far, split_axis=0, concat_axis=0, tiled=True)  13.6 us
    select_n x2, other arithmetic, body(): jnp.take(spread, slot_of, axis=0)  13 us
    gather x1, local copies, waits for them, and re-layouts, body(): jnp.take(spread, slot_of, axis=0)  11.3 us
    all_to_all x1, blocking collectives, sent_to_all(): return lax.all_to_all(copies, axis, split_axis=0, concat_axis=0, tiled=True)  10.6 us
    all_to_all x1, waiting for transfers between devices, sent_to_all(): return lax.all_to_all(copies, axis, split_axis=0, concat_axis=0, tiled=True)  8.38 us
  transfers between devices with their start and end apart: 2, of which 2 were waited for; matrix products, arithmetic and copies ran while one was open for 1% of the time, Pallas kernels for 0%

commit v1 on v0

v1 whole, which is shorter than its diff:
```python
import functools

import jax
import jax.numpy as jnp
from jax import lax
from jax.experimental import pallas as pl
from jax.experimental.pallas import tpu as pltpu
from jax.sharding import PartitionSpec as P

MESH = pl.DeviceIdType.MESH
LANES = 128
ROWS = 16
MATS = 3
CHUNKS = 2
PART = ROWS // CHUNKS


def whole_wait(ref, sem):
    pltpu.make_async_copy(ref, ref, sem).wait()


def kernel(
    ns,
    nz,
    cap,
    nb,
    starts,
    mats,
    step,
    grad_hbm,
    param_hbm,
    row_state,
    col_state,
    out_hbm,
    out_rows,
    out_cols,
    g,
    p,
    stat,
    from_plane,
    mine,
    from_line,
    totals,
    row_inv,
    row_fac,
    col_fac,
    updated,
    arrived_0,
    arrived_1,
    pieces,
    slot_of,
    weight,
    matrix_of,
    load_sem,
    small_send,
    small_recv,
    swap_send,
    swap_recv,
    ring_send,
    ring_recv,
    store_sem,
):
    me = lax.axis_index("shard")
    z = lax.axis_index("dp")
    cols = ns * LANES
    f32 = jnp.float32
    half = nb // 2
    last = nz // 2 - 1
    arrived = (arrived_0, arrived_1)

    loads = [pltpu.make_async_copy(grad_hbm, g, load_sem.at[0]), pltpu.make_async_copy(param_hbm, p, load_sem.at[1])]
    for load in loads:
        load.start()
    barrier = pltpu.get_barrier_semaphore()

    @pl.loop(1, ns)
    def _(k):
        pl.semaphore_signal(barrier, inc=1, device_id={"shard": lax.rem(me + k, ns)}, device_id_type=MESH)

    @pl.loop(1, nz)
    def _(k):
        pl.semaphore_signal(barrier, inc=1, device_id={"dp": lax.rem(z + k, nz)}, device_id_type=MESH)

    first = starts[me]
    owned = jnp.where(me == ns - 1, nb, starts[jnp.minimum(me + 1, ns - 1)]) - first
    for j in range(cap):
        m_of = jnp.clip(mats[jnp.minimum(first + j, nb - 1)], 0, MATS - 1)
        matrix_of[j] = m_of
        for m in range(MATS):
            weight[j * MATS + m] = jnp.where((j < owned) & (m_of == m), 1.0, 0.0).astype(f32)

    def place(b, owner):
        following = starts[jnp.minimum(owner + 1, ns - 1)]
        owner = jnp.where((owner < ns - 1) & (following <= b), owner + 1, owner)
        slot_of[b] = owner * cap + jnp.clip(b - starts[owner], 0, cap - 1)
        return owner

    lax.fori_loop(0, nb, place, jnp.int32(0))

    t = jnp.full((ROWS, LANES), step[0].astype(f32), f32)
    beta = 1.0 - jnp.exp(-0.8 * jnp.log(t))
    rest = 1.0 - beta
    lr = 1.0 / jnp.sqrt(jnp.maximum(t, 10000.0))
    sub = lax.broadcasted_iota(jnp.int32, (ROWS, ROWS), 0)
    lane = lax.broadcasted_iota(jnp.int32, (ROWS, ROWS), 1)
    eye = sub == lane

    loads[0].wait()
    row_sums = [jnp.zeros((ROWS, 1), f32) for _ in range(MATS)]
    for j in range(cap):
        gj = g[j]
        total = jnp.sum(gj * gj, axis=1, keepdims=True)
        live = jnp.full((ROWS, 1), owned, jnp.int32) > j
        old = jnp.sum(jnp.where(eye, jnp.broadcast_to(row_state[j : j + 1, :], (ROWS, ROWS)), 0.0), axis=1, keepdims=True)
        new = jnp.where(live, beta[:, :1] * old + rest[:, :1] * total / cols, 0.0)
        safe = jnp.where(live, new, 1.0)
        row_inv[j] = jnp.broadcast_to(1.0 / safe, (ROWS, LANES))
        row_fac[j] = jnp.broadcast_to(1.0 / jnp.sqrt(safe), (ROWS, LANES))
        out_rows[j : j + 1, :] = jnp.sum(jnp.where(eye, jnp.broadcast_to(new, (ROWS, ROWS)), 0.0), axis=0, keepdims=True)
        for m in range(MATS):
            row_sums[m] = row_sums[m] + weight[j * MATS + m] * new
    at_lane = lax.broadcasted_iota(jnp.int32, (1, LANES), 1)
    row_line = jnp.zeros((1, LANES), f32)
    for m in range(MATS):
        row_line = jnp.where(at_lane == m, jnp.sum(row_sums[m], axis=0, keepdims=True), row_line)

    @pl.loop(0, ns)
    def _(q):
        at = pl.ds(pl.multiple_of(q * LANES, LANES), LANES)
        acc = [jnp.zeros((8, LANES), f32) for _ in range(2 * MATS)]
        for j in range(cap):
            upper = g[j, 0:8, at]
            lower = g[j, 8:16, at]
            upper, lower = upper * upper, lower * lower
            plain = upper + lower
            quot = upper * row_inv[j, 0:8] + lower * row_inv[j, 8:16]
            for m in range(MATS):
                w = weight[j * MATS + m]
                acc[m] = acc[m] + w * plain
                acc[MATS + m] = acc[MATS + m] + w * quot
        for i in range(2 * MATS):
            stat[q, i : i + 1, :] = jnp.sum(acc[i], axis=0, keepdims=True)
        stat[q, 6:7, :] = row_line
        stat[q, 7:8, :] = jnp.zeros((1, LANES), f32)

    pl.semaphore_wait(barrier, ns - 1 + nz - 1)

    from_plane[me] = stat[me]

    @pl.loop(1, ns)
    def _(k):
        q = lax.rem(me + k, ns)
        pltpu.make_async_remote_copy(
            stat.at[q], from_plane.at[me], small_send.at[0], small_recv.at[0], device_id={"shard": q}, device_id_type=MESH
        ).start()

    whole_wait(from_plane.at[pl.ds(0, ns - 1)], small_recv.at[0])
    parts = [from_plane[s] for s in range(4)]
    for s in range(4, ns):
        parts[s % 4] = parts[s % 4] + from_plane[s]
    mine[0] = (parts[0] + parts[1]) + (parts[2] + parts[3])
    from_line[z] = mine[0]

    @pl.loop(1, nz)
    def _(k):
        other = lax.rem(z + k, nz)
        pltpu.make_async_remote_copy(
            mine.at[0], from_line.at[z], small_send.at[1], small_recv.at[1], device_id={"dp": other}, device_id_type=MESH
        ).start()

    whole_wait(from_line.at[pl.ds(0, nz - 1)], small_recv.at[1])
    both = from_line[0]
    for s in range(1, nz):
        both = both + from_line[s]
    mine[1] = both
    totals[me] = both

    @pl.loop(1, ns)
    def _(k):
        q = lax.rem(me + k, ns)
        pltpu.make_async_remote_copy(
            mine.at[1], totals.at[me], small_send.at[2], small_recv.at[2], device_id={"shard": q}, device_id_type=MESH
        ).start()

    loads[1].wait()
    whole_wait(totals.at[pl.ds(0, ns - 1)], small_recv.at[2])

    row_count = jnp.where(lax.broadcasted_iota(jnp.int32, (MATS, LANES), 0) < 2, f32(cols), f32(nb * ROWS * nz - 2 * cols))
    ratio = jnp.zeros((MATS, LANES), f32)
    for q in range(ns):
        at = pl.ds(q * LANES, LANES)
        new = beta[:MATS] * col_state[:, at] + rest[:MATS] * totals[q, 0:MATS, :] / row_count
        out_cols[:, at] = new
        ratio = ratio + totals[q, MATS : 2 * MATS, :] / new
    ratio = jnp.sum(ratio, axis=1, keepdims=True)
    spread = jnp.broadcast_to(totals[0, 6:7, :], (8, LANES))
    on = lax.broadcasted_iota(jnp.int32, (8, LANES), 0) == lax.broadcasted_iota(jnp.int32, (8, LANES), 1)
    row_total = jnp.sum(jnp.where(on, spread, 0.0), axis=1, keepdims=True)[:MATS]
    average = row_total / row_count[:, :1]
    clip = jnp.maximum(1.0, jnp.sqrt(average * ratio / (row_count[:, :1] * cols)))
    scale = lr[:MATS, :1] * jnp.sqrt(average) / clip
    for q in range(ns):
        col_fac[q, 0:MATS, :] = scale / jnp.sqrt(out_cols[:, pl.ds(q * LANES, LANES)])

    @pl.loop(0, ns)
    def _(q):
        at = pl.ds(pl.multiple_of(q * LANES, LANES), LANES)
        for j in range(cap):
            factor = col_fac[q, pl.ds(matrix_of[j], 1), :]
            value = p[j, :, at].astype(f32) - g[j, :, at] * row_fac[j] * factor
            for c in range(CHUNKS):
                updated[c, q, j] = value[c * PART : (c + 1) * PART].astype(jnp.bfloat16)

    for c in range(CHUNKS):

        @pl.loop(1, ns)
        def _(k):
            q = lax.rem(me + k, ns)
            pltpu.make_async_remote_copy(
                updated.at[c, q],
                arrived[c].at[pl.ds(me * cap, cap)],
                swap_send.at[c],
                swap_recv.at[c],
                device_id={"shard": q},
                device_id_type=MESH,
            ).start()

        for j in range(cap):
            arrived[c][me * cap + j] = updated[c, me, j]

    def unit(c, origin, h):
        return pieces.at[c * nz + origin, pl.ds(h * half, half)]

    def ring_copy(way, c, s, h):
        origin = lax.rem(z + (nz - s if way == 0 else s), nz)
        to = lax.rem(z + (1 if way == 0 else nz - 1), nz)
        return pltpu.make_async_remote_copy(
            unit(c, origin, h),
            unit(c, origin, h),
            ring_send.at[way],
            ring_recv.at[way, c, s, h],
            device_id={"dp": to},
            device_id_type=MESH,
        )

    def keep(c, origin, h):
        pltpu.make_async_copy(unit(c, origin, h), out_hbm.at[pl.ds(h * half, half), origin, c], store_sem.at[0]).start()

    def compact(c):
        whole_wait(arrived[c].at[pl.ds(0, (ns - 1) * cap)], swap_recv.at[c])
        for h in range(2):

            @pl.loop(h * half, (h + 1) * half, unroll=8)
            def _(b):
                pieces[c * nz + z, b] = arrived[c][slot_of[b]]

            ring_copy(0, c, 0, h).start()
            ring_copy(1, c, 0, h).start()
            keep(c, z, h)

    def take(c, s):
        for h in range(2):
            for way in range(2):
                if s == last and h != way:
                    continue
                origin = lax.rem(z + (nz - 1 - s if way == 0 else 1 + s), nz)
                whole_wait(unit(c, origin, h), ring_recv.at[way, c, s, h])
                if s + 1 < last or (s + 1 == last and h == way):
                    ring_copy(way, c, s + 1, h).start()
                keep(c, origin, h)

    compact(0)
    take(0, 0)
    for c in range(1, CHUNKS):
        compact(c)
        for s in range(1, last + 1):
            take(c - 1, s)
        take(c, 0)
    for s in range(1, last + 1):
        take(CHUNKS - 1, s)

    whole_wait(from_plane.at[pl.ds(0, ns - 1)], small_send.at[0])
    whole_wait(from_line.at[pl.ds(0, nz - 1)], small_send.at[1])
    whole_wait(from_plane.at[pl.ds(0, ns - 1)], small_send.at[2])
    for c in range(CHUNKS):
        whole_wait(arrived[c].at[pl.ds(0, (ns - 1) * cap)], swap_send.at[c])
    for way in range(2):
        whole_wait(pieces.at[pl.ds(0, CHUNKS * last + CHUNKS // 2)], ring_send.at[way])
    whole_wait(out_hbm, store_sem.at[0])


def body(ns, nz, grad, param, row_state, col_state, block_start, block_matrix, step):
    cap = grad.shape[0]
    nb = block_matrix.shape[0]
    f32, bf16 = jnp.float32, jnp.bfloat16
    dma = pltpu.SemaphoreType.DMA
    smem = pl.BlockSpec(memory_space=pltpu.SMEM)
    vmem = pl.BlockSpec(memory_space=pltpu.VMEM)
    anywhere = pl.BlockSpec(memory_space=pl.ANY)
    new_params, new_rows, new_cols = pl.pallas_call(
        functools.partial(kernel, ns, nz, cap, nb),
        out_shape=(
            jax.ShapeDtypeStruct((nb, nz, CHUNKS, PART, LANES), bf16),
            jax.ShapeDtypeStruct(row_state.shape, f32),
            jax.ShapeDtypeStruct(col_state.shape, f32),
        ),
        in_specs=[smem, smem, smem, anywhere, anywhere, vmem, vmem],
        out_specs=(anywhere, vmem, vmem),
        scratch_shapes=[
            pltpu.VMEM(grad.shape, f32),
            pltpu.VMEM(param.shape, bf16),
            pltpu.VMEM((ns, 8, LANES), f32),
            pltpu.VMEM((ns, 8, LANES), f32),
            pltpu.VMEM((2, 8, LANES), f32),
            pltpu.VMEM((nz, 8, LANES), f32),
            pltpu.VMEM((ns, 8, LANES), f32),
            pltpu.VMEM((cap, ROWS, LANES), f32),
            pltpu.VMEM((cap, ROWS, LANES), f32),
            pltpu.VMEM((ns, 8, LANES), f32),
            pltpu.VMEM((CHUNKS, ns, cap, PART, LANES), bf16),
            pltpu.VMEM((ns * cap, PART, LANES), bf16),
            pltpu.VMEM((ns * cap, PART, LANES), bf16),
            pltpu.VMEM((CHUNKS * nz, nb, PART, LANES), bf16),
            pltpu.SMEM((nb,), jnp.int32),
            pltpu.SMEM((cap * MATS,), f32),
            pltpu.SMEM((cap,), jnp.int32),
            dma((2,)),
            dma((3,)),
            dma((3,)),
            dma((CHUNKS,)),
            dma((CHUNKS,)),
            dma((2,)),
            dma((2, CHUNKS, nz // 2, 2)),
            dma((1,)),
        ],
        compiler_params=pltpu.CompilerParams(collective_id=0, has_side_effects=True),
        name="step",
    )(block_start, block_matrix, step, grad, param, row_state, col_state)
    return new_params.reshape(nb * nz * ROWS, LANES), new_rows, new_cols


def solution(mesh):
    return jax.shard_map(
        functools.partial(body, mesh.shape["shard"], mesh.shape["dp"]),
        mesh=mesh,
        in_specs=(P("shard", "dp", None), P("shard", "dp", None), P("shard", "dp"), P(), P(), P(), P()),
        out_specs=(P(None, "shard"), P("shard", "dp"), P()),
        check_vma=False,
    )
```

time: 265 us -> 99.8 us (0.38)
  waiting for transfers between devices: 110 us -> 0 us
  Pallas kernels: 0 us -> 90.9 us
  blocking collectives: 68.3 us -> 0 us
  other arithmetic: 25.5 us -> 0 us
  local copies, waits for them, and re-layouts: 31.3 us -> 6.67 us
  between operations: 16.3 us -> 1.3 us
  matrix products: 7.16 us -> 0 us
  starting transfers between devices: 4.21 us -> 0 us
    all_gather x1 -> x0, waiting for transfers between devices: 102 us -> none  [body(): spread = lax.all_gather(column_rows, 'dp', axis=1, tiled=True)]
    pallas_call x0 -> x1, Pallas kernels: none -> 90.9 us  [body(): pl.pallas_call(functools.partial(kernel, ns, nz, cap, nb), out_shape=(jax...]
    all_to_all x5 -> x0, blocking collectives: 68.3 us -> none  [the longest x2 27.2 us: moved_by_axis(): lax.all_to_all(blocks, axes[k], split_axis=k, concat_axis=k, tiled=True)]
    select_n x5 -> x0, other arithmetic: 13.1 us -> none  [the longest x2 13 us: body(): jnp.take(spread, slot_of, axis=0)]
    gather x2 -> x0, local copies, waits for them, and re-layouts: 12.9 us -> none  [the longest x1 11.3 us: body(): jnp.take(spread, slot_of, axis=0)]
    all_to_all x1 -> x0, waiting for transfers between devices: 8.38 us -> none  [sent_to_all(): return lax.all_to_all(copies, axis, split_axis=0, concat_axis=0, tiled=True)]
    reduce_sum x8 -> x0, other arithmetic: 8.1 us -> none  [the longest x1 1.89 us: body(): jnp.sum(squares, axis=2)]
    dot_general x6 -> x0, matrix products: 7.16 us -> none  [the longest x1 1.97 us: body(): jnp.einsum('sm,sd->md', member, jnp.sum(squares, axis=1), precision=lax.P...]
  transfers between devices with their start and end apart: 2 -> 0, of which waited for: 2 -> 0; matrix products, arithmetic and copies ran while one was open for 1% -> 0% of each run, Pallas kernels for 0% -> 0%
where the time goes in v1:
time: 99.8 us; the launch traced here: 98.9 us
  Pallas kernels  90.9 us (91%)
  local copies, waits for them, and re-layouts  6.67 us (7%)
  between operations  1.3 us (1%)
    pallas_call x1, Pallas kernels, body(): pl.pallas_call(functools.partial(kernel, ns, nz, cap, nb), out_shape=(jax...  90.9 us
    unnamed x7, local copies, waits for them, and re-layouts  6.67 us

profile of v1, /device:TPU:2, one launch (start us, length us, event | category | flops | bytes accessed | tf_op | source)
XLA Modules:
  0.0 98.9 jit_solution(14058116737200978191)
XLA Ops:
  1.3 90.9 %step.2 = (bf16[144,8,2,8,128]{4,3,2,1,0:T(8,128)(2,1)}, f32[9,16]{1,0:T(8,128)}, f32[3,4096]{1,0:T(4,128)}) custom-call(s32[32]{0:T(128)} %starts.1, s32[144]{0:T(256)} %mats.1, s32[1]{0:T(128)S(6)} %copy.13.step, f32[9,16,4096]{2,1,0:T(8,128)} %grad_hbm.1, bf16[9,16,4096]{2,1,0:T(8,128)(2,1)} %param_hbm.1, f32[9,16]{1,0:T(8,128)} %row_state.1, ...), custom_call_target="tpu_custom_call" | custom-call | tf_op jit(solution)/shard_map/step/pallas_call | solution.py:300
  92.2 0.0 copy-start.1
  92.2 0.0 copy-start
  92.2 5.4 %copy.14 = bf16[18432,128]{1,0:T(8,128)(2,1)} copy(bf16[18432,128]{1,0:T(8,128)(2,1)} %bitcast.1) | data formatting | bytes 9437184
  97.6 0.0 copy-done.1
  97.6 0.6 copy.15
  98.2 0.0 copy-done
  98.2 0.6 copy.16
Async XLA Ops:
  92.2 5.5 %copy-start.1 = (f32[9,16]{1,0:T(8,128)S(1)}, f32[9,16]{1,0:T(8,128)}, u32[]{:S(2)}) copy-start(f32[9,16]{1,0:T(8,128)} %get-tuple-element.13) | copy-start | bytes 1732
  92.2 6.0 %copy-start = (f32[3,4096]{1,0:T(4,128)S(1)}, f32[3,4096]{1,0:T(4,128)}, u32[]{:S(2)}) copy-start(f32[3,4096]{1,0:T(4,128)} %get-tuple-element.14) | copy-start | bytes 147460

commit v2 on v1

--- a/solution.py
+++ b/solution.py
@@ -11,12 +11,17 @@
 LANES = 128
 ROWS = 16
 MATS = 3
-CHUNKS = 2
+CHUNKS = 4
 PART = ROWS // CHUNKS
 
 
 def whole_wait(ref, sem):
     pltpu.make_async_copy(ref, ref, sem).wait()
+
+
+def sends(last):
+    order = [(c, s) for c in range(CHUNKS) for s in range(last + 1)]
+    return sorted(order, key=lambda at: (at[0] * (last + 1) + at[1] - (1.5 if at[1] == 0 else 0), at))
 
 
 def kernel(
@@ -24,16 +29,20 @@
     nz,
     cap,
     nb,
+    step,
+    starts_hbm,
+    mats_hbm,
+    grad_hbm,
+    param_hbm,
+    row_state_hbm,
+    col_state_hbm,
+    pieces,
+    out_rows,
+    out_cols,
     starts,
     mats,
-    step,
-    grad_hbm,
-    param_hbm,
     row_state,
     col_state,
-    out_hbm,
-    out_rows,
-    out_cols,
     g,
     p,
     stat,
@@ -47,7 +56,8 @@
     updated,
     arrived_0,
     arrived_1,
-    pieces,
+    arrived_2,
+    arrived_3,
     slot_of,
     weight,
     matrix_of,
@@ -58,7 +68,6 @@
     swap_recv,
     ring_send,
     ring_recv,
-    store_sem,
 ):
     me = lax.axis_index("shard")
     z = lax.axis_index("dp")
@@ -66,9 +75,21 @@
     f32 = jnp.float32
     half = nb // 2
     last = nz // 2 - 1
-    arrived = (arrived_0, arrived_1)
-
-    loads = [pltpu.make_async_copy(grad_hbm, g, load_sem.at[0]), pltpu.make_async_copy(param_hbm, p, load_sem.at[1])]
+    arrived = (arrived_0, arrived_1, arrived_2, arrived_3)
+
+    loads = [
+        pltpu.make_async_copy(source, target, load_sem.at[i])
+        for i, (source, target) in enumerate(
+            (
+                (starts_hbm, starts),
+                (mats_hbm, mats),
+                (row_state_hbm, row_state),
+                (grad_hbm, g),
+                (col_state_hbm, col_state),
+                (param_hbm, p),
+            )
+        )
+    ]
     for load in loads:
         load.start()
     barrier = pltpu.get_barrier_semaphore()
@@ -81,6 +102,8 @@
     def _(k):
         pl.semaphore_signal(barrier, inc=1, device_id={"dp": lax.rem(z + k, nz)}, device_id_type=MESH)
 
+    for load in loads[:3]:
+        load.wait()
     first = starts[me]
     owned = jnp.where(me == ns - 1, nb, starts[jnp.minimum(me + 1, ns - 1)]) - first
     for j in range(cap):
@@ -89,14 +112,6 @@
         for m in range(MATS):
             weight[j * MATS + m] = jnp.where((j < owned) & (m_of == m), 1.0, 0.0).astype(f32)
 
-    def place(b, owner):
-        following = starts[jnp.minimum(owner + 1, ns - 1)]
-        owner = jnp.where((owner < ns - 1) & (following <= b), owner + 1, owner)
-        slot_of[b] = owner * cap + jnp.clip(b - starts[owner], 0, cap - 1)
-        return owner
-
-    lax.fori_loop(0, nb, place, jnp.int32(0))
-
     t = jnp.full((ROWS, LANES), step[0].astype(f32), f32)
     beta = 1.0 - jnp.exp(-0.8 * jnp.log(t))
     rest = 1.0 - beta
@@ -105,7 +120,7 @@
     lane = lax.broadcasted_iota(jnp.int32, (ROWS, ROWS), 1)
     eye = sub == lane
 
-    loads[0].wait()
+    loads[3].wait()
     row_sums = [jnp.zeros((ROWS, 1), f32) for _ in range(MATS)]
     for j in range(cap):
         gj = g[j]
@@ -154,6 +169,14 @@
             stat.at[q], from_plane.at[me], small_send.at[0], small_recv.at[0], device_id={"shard": q}, device_id_type=MESH
         ).start()
 
+    def place(b, owner):
+        following = starts[jnp.minimum(owner + 1, ns - 1)]
+        owner = jnp.where((owner < ns - 1) & (following <= b), owner + 1, owner)
+        slot_of[b] = owner * cap + jnp.clip(b - starts[owner], 0, cap - 1)
+        return owner
+
+    lax.fori_loop(0, nb, place, jnp.int32(0))
+
     whole_wait(from_plane.at[pl.ds(0, ns - 1)], small_recv.at[0])
     parts = [from_plane[s] for s in range(4)]
     for s in range(4, ns):
@@ -182,7 +205,8 @@
             mine.at[1], totals.at[me], small_send.at[2], small_recv.at[2], device_id={"shard": q}, device_id_type=MESH
         ).start()
 
-    loads[1].wait()
+    loads[4].wait()
+    loads[5].wait()
     whole_wait(totals.at[pl.ds(0, ns - 1)], small_recv.at[2])
 
     row_count = jnp.where(lax.broadcasted_iota(jnp.int32, (MATS, LANES), 0) < 2, f32(cols), f32(nb * ROWS * nz - 2 * cols))
@@ -243,9 +267,6 @@
             device_id_type=MESH,
         )
 
-    def keep(c, origin, h):
-        pltpu.make_async_copy(unit(c, origin, h), out_hbm.at[pl.ds(h * half, half), origin, c], store_sem.at[0]).start()
-
     def compact(c):
         whole_wait(arrived[c].at[pl.ds(0, (ns - 1) * cap)], swap_recv.at[c])
         for h in range(2):
@@ -256,7 +277,6 @@
 
             ring_copy(0, c, 0, h).start()
             ring_copy(1, c, 0, h).start()
-            keep(c, z, h)
 
     def take(c, s):
         for h in range(2):
@@ -267,17 +287,14 @@
                 whole_wait(unit(c, origin, h), ring_recv.at[way, c, s, h])
                 if s + 1 < last or (s + 1 == last and h == way):
                     ring_copy(way, c, s + 1, h).start()
-                keep(c, origin, h)
-
-    compact(0)
-    take(0, 0)
-    for c in range(1, CHUNKS):
-        compact(c)
-        for s in range(1, last + 1):
-            take(c - 1, s)
-        take(c, 0)
-    for s in range(1, last + 1):
-        take(CHUNKS - 1, s)
+
+    for c, s in sends(last):
+        if s == 0:
+            compact(c)
+        else:
+            take(c, s - 1)
+    for c in range(CHUNKS):
+        take(c, last)
 
     whole_wait(from_plane.at[pl.ds(0, ns - 1)], small_send.at[0])
     whole_wait(from_line.at[pl.ds(0, nz - 1)], small_send.at[1])
@@ -286,7 +303,18 @@
         whole_wait(arrived[c].at[pl.ds(0, (ns - 1) * cap)], swap_send.at[c])
     for way in range(2):
         whole_wait(pieces.at[pl.ds(0, CHUNKS * last + CHUNKS // 2)], ring_send.at[way])
-    whole_wait(out_hbm, store_sem.at[0])
+
+
+def finish(nz, pieces, rows, cols, out_params, out_rows, out_cols, sem):
+    copies = [
+        pltpu.make_async_copy(pieces.at[c * nz + s], out_params.at[:, s, c], sem.at[c * nz + s]) for c in range(CHUNKS) for s in range(nz)
+    ]
+    copies.append(pltpu.make_async_copy(rows, out_rows, sem.at[CHUNKS * nz]))
+    copies.append(pltpu.make_async_copy(cols, out_cols, sem.at[CHUNKS * nz + 1]))
+    for copy in copies:
+        copy.start()
+    for copy in copies:
+        copy.wait()
 
 
 def body(ns, nz, grad, param, row_state, col_state, block_start, block_matrix, step):
@@ -294,19 +322,22 @@
     nb = block_matrix.shape[0]
     f32, bf16 = jnp.float32, jnp.bfloat16
     dma = pltpu.SemaphoreType.DMA
-    smem = pl.BlockSpec(memory_space=pltpu.SMEM)
     vmem = pl.BlockSpec(memory_space=pltpu.VMEM)
-    anywhere = pl.BlockSpec(memory_space=pl.ANY)
-    new_params, new_rows, new_cols = pl.pallas_call(
+    hbm = pl.BlockSpec(memory_space=pltpu.HBM)
+    landed = pl.pallas_call(
         functools.partial(kernel, ns, nz, cap, nb),
         out_shape=(
-            jax.ShapeDtypeStruct((nb, nz, CHUNKS, PART, LANES), bf16),
-            jax.ShapeDtypeStruct(row_state.shape, f32),
-            jax.ShapeDtypeStruct(col_state.shape, f32),
+            pltpu.VMEM((CHUNKS * nz, nb, PART, LANES), bf16),
+            pltpu.VMEM(row_state.shape, f32),
+            pltpu.VMEM(col_state.shape, f32),
         ),
-        in_specs=[smem, smem, smem, anywhere, anywhere, vmem, vmem],
-        out_specs=(anywhere, vmem, vmem),
+        in_specs=[pl.BlockSpec(memory_space=pltpu.SMEM)] + [hbm] * 6,
+        out_specs=(vmem, vmem, vmem),
         scratch_shapes=[
+            pltpu.SMEM(block_start.shape, jnp.int32),
+            pltpu.SMEM(block_matrix.shape, jnp.int32),
+            pltpu.VMEM(row_state.shape, f32),
+            pltpu.VMEM(col_state.shape, f32),
             pltpu.VMEM(grad.shape, f32),
             pltpu.VMEM(param.shape, bf16),
             pltpu.VMEM((ns, 8, LANES), f32),
@@ -318,24 +349,34 @@
             pltpu.VMEM((cap, ROWS, LANES), f32),
             pltpu.VMEM((ns, 8, LANES), f32),
             pltpu.VMEM((CHUNKS, ns, cap, PART, LANES), bf16),
-            pltpu.VMEM((ns * cap, PART, LANES), bf16),
-            pltpu.VMEM((ns * cap, PART, LANES), bf16),
-            pltpu.VMEM((CHUNKS * nz, nb, PART, LANES), bf16),
+            *[pltpu.VMEM((ns * cap, PART, LANES), bf16) for _ in range(CHUNKS)],
             pltpu.SMEM((nb,), jnp.int32),
             pltpu.SMEM((cap * MATS,), f32),
             pltpu.SMEM((cap,), jnp.int32),
-            dma((2,)),
+            dma((6,)),
             dma((3,)),
             dma((3,)),
             dma((CHUNKS,)),
             dma((CHUNKS,)),
             dma((2,)),
             dma((2, CHUNKS, nz // 2, 2)),
-            dma((1,)),
         ],
-        compiler_params=pltpu.CompilerParams(collective_id=0, has_side_effects=True),
+        compiler_params=pltpu.CompilerParams(collective_id=0, has_side_effects=True, vmem_limit_bytes=24 << 20),
         name="step",
-    )(block_start, block_matrix, step, grad, param, row_state, col_state)
+    )(step, *(pltpu.with_memory_space_constraint(a, pltpu.HBM) for a in (block_start, block_matrix, grad, param, row_state, col_state)))
+    new_params, new_rows, new_cols = pl.pallas_call(
+        functools.partial(finish, nz),
+        out_shape=(
+            jax.ShapeDtypeStruct((nb, nz, CHUNKS, PART, LANES), bf16),
+            jax.ShapeDtypeStruct(row_state.shape, f32),
+            jax.ShapeDtypeStruct(col_state.shape, f32),
+        ),
+        in_specs=[vmem] * 3,
+        out_specs=(hbm,) * 3,
+        scratch_shapes=[dma((CHUNKS * nz + 2,))],
+        compiler_params=pltpu.CompilerParams(vmem_limit_bytes=8 << 20),
+        name="finish",
+    )(*landed)
     return new_params.reshape(nb * nz * ROWS, LANES), new_rows, new_cols
 
 

time: 99.8 us -> 90.2 us (0.904)
  local copies, waits for them, and re-layouts: 6.67 us -> 0 us
  Pallas kernels: 90.9 us -> 87.3 us
    unnamed x7 -> x0, local copies, waits for them, and re-layouts: 6.67 us -> none
    pallas_call x1 -> x2, Pallas kernels: 90.9 us -> 87.3 us  [the longest x1 84.8 us: body(): pl.pallas_call(functools.partial(kernel, ns, nz, cap, nb), out_shape=(plt...]
where the time goes in v2:
time: 90.2 us; the launch traced here: 88.6 us
  Pallas kernels  87.3 us (97%)
  between operations  1.29 us (1%)
    pallas_call x1, Pallas kernels, body(): pl.pallas_call(functools.partial(kernel, ns, nz, cap, nb), out_shape=(plt...  84.8 us
    pallas_call x1, Pallas kernels, body(): pl.pallas_call(functools.partial(finish, nz), out_shape=(jax.ShapeDtypeSt...  2.48 us

profile of v2, /device:TPU:2, one launch (start us, length us, event | category | flops | bytes accessed | tf_op | source)
XLA Modules:
  0.0 88.6 jit_solution(6399072397020670098)
XLA Ops:
  1.3 84.8 %step.2 = (bf16[32,144,4,128]{3,2,1,0:T(4,128)(2,1)S(1)}, f32[9,16]{1,0:T(8,128)S(1)}, f32[3,4096]{1,0:T(4,128)S(1)}) custom-call(s32[1]{0:T(128)S(6)} %copy.10.step, s32[32]{0:T(128)} %starts_hbm.1, s32[144]{0:T(256)} %mats_hbm.1, f32[9,16,4096]{2,1,0:T(8,128)} %grad_hbm.1, bf16[9,16,4096]{2,1,0:T(8,128)(2,1)} %param_hbm.1, f32[9,16]{1,0:T(8,128)} %row_state_hbm.1, ...), custom_call_target="tpu_custom_call" | custom-call | tf_op jit(solution)/shard_map/step/pallas_call | solution.py:327
  86.1 2.5 %finish.1 = (bf16[144,8,4,4,128]{4,3,2,1,0:T(4,128)(2,1)}, f32[9,16]{1,0:T(8,128)}, f32[3,4096]{1,0:T(4,128)}) custom-call(bf16[32,144,4,128]{3,2,1,0:T(4,128)(2,1)S(1)} %get-tuple-element.9.pieces, f32[9,16]{1,0:T(8,128)S(1)} %get-tuple-element.10.rows, f32[3,4096]{1,0:T(4,128)S(1)} %get-tuple-element.11.cols), custom_call_target="tpu_custom_call" | custom-call | tf_op jit(solution)/shard_map/finish/pallas_call | solution.py:367

commit v3 on v2

--- a/solution.py
+++ b/solution.py
@@ -12,6 +12,9 @@
 ROWS = 16
 MATS = 3
 CHUNKS = 4
+UNITS = 4
+UNROLL = 6
+LATE = 6
 PART = ROWS // CHUNKS
 
 
@@ -21,7 +24,7 @@
 
 def sends(last):
     order = [(c, s) for c in range(CHUNKS) for s in range(last + 1)]
-    return sorted(order, key=lambda at: (at[0] * (last + 1) + at[1] - (1.5 if at[1] == 0 else 0), at))
+    return sorted(order, key=lambda at: (3.5 * at[0] + 2 * at[1] - 0.5 if at[0] else at[1] + max(0, at[1] - 2), at))
 
 
 def kernel(
@@ -54,7 +57,10 @@
     row_fac,
     col_fac,
     updated,
-    arrived_0,
+    early_g,
+    early_p,
+    came_g,
+    came_p,
     arrived_1,
     arrived_2,
     arrived_3,
@@ -73,9 +79,9 @@
     z = lax.axis_index("dp")
     cols = ns * LANES
     f32 = jnp.float32
-    half = nb // 2
+    span = nb // UNITS
     last = nz // 2 - 1
-    arrived = (arrived_0, arrived_1, arrived_2, arrived_3)
+    arrived = (None, arrived_1, arrived_2, arrived_3)
 
     loads = [
         pltpu.make_async_copy(source, target, load_sem.at[i])
@@ -169,6 +175,34 @@
             stat.at[q], from_plane.at[me], small_send.at[0], small_recv.at[0], device_id={"shard": q}, device_id_type=MESH
         ).start()
 
+    loads[5].wait()
+
+    def early(q):
+        now = cap - LATE
+        parts = ((early_g.at[q], me * cap, cap, came_g), (early_p.at[q, pl.ds(0, now)], me * cap, now, came_p))
+        parts += ((early_p.at[q, pl.ds(now, LATE)], me * cap + now, LATE, came_p),)
+        return [
+            pltpu.make_async_remote_copy(
+                source, target.at[pl.ds(at, size)], swap_send.at[i], swap_recv.at[i], device_id={"shard": q}, device_id_type=MESH
+            )
+            for i, (source, at, size, target) in enumerate(parts)
+        ]
+
+    def prepare(q, to_g, to_p, first_row):
+        at = pl.ds(pl.multiple_of(q * LANES, LANES), LANES)
+        for j in range(cap):
+            to_g[first_row + j] = (g[j, 0:8, at] * row_fac[j, 0:8])[:PART]
+            to_p[first_row + j] = p[j, :, at][:PART]
+
+    prepare(me, came_g, came_p, me * cap)
+
+    @pl.loop(1, ns)
+    def _(k):
+        q = lax.rem(me + k, ns)
+        prepare(q, early_g.at[q], early_p.at[q], 0)
+        for copy in early(q)[:2]:
+            copy.start()
+
     def place(b, owner):
         following = starts[jnp.minimum(owner + 1, ns - 1)]
         owner = jnp.where((owner < ns - 1) & (following <= b), owner + 1, owner)
@@ -205,8 +239,11 @@
             mine.at[1], totals.at[me], small_send.at[2], small_recv.at[2], device_id={"shard": q}, device_id_type=MESH
         ).start()
 
+    @pl.loop(1, ns)
+    def _(k):
+        early(lax.rem(me + k, ns))[2].start()
+
     loads[4].wait()
-    loads[5].wait()
     whole_wait(totals.at[pl.ds(0, ns - 1)], small_recv.at[2])
 
     row_count = jnp.where(lax.broadcasted_iota(jnp.int32, (MATS, LANES), 0) < 2, f32(cols), f32(nb * ROWS * nz - 2 * cols))
@@ -226,34 +263,8 @@
     for q in range(ns):
         col_fac[q, 0:MATS, :] = scale / jnp.sqrt(out_cols[:, pl.ds(q * LANES, LANES)])
 
-    @pl.loop(0, ns)
-    def _(q):
-        at = pl.ds(pl.multiple_of(q * LANES, LANES), LANES)
-        for j in range(cap):
-            factor = col_fac[q, pl.ds(matrix_of[j], 1), :]
-            value = p[j, :, at].astype(f32) - g[j, :, at] * row_fac[j] * factor
-            for c in range(CHUNKS):
-                updated[c, q, j] = value[c * PART : (c + 1) * PART].astype(jnp.bfloat16)
-
-    for c in range(CHUNKS):
-
-        @pl.loop(1, ns)
-        def _(k):
-            q = lax.rem(me + k, ns)
-            pltpu.make_async_remote_copy(
-                updated.at[c, q],
-                arrived[c].at[pl.ds(me * cap, cap)],
-                swap_send.at[c],
-                swap_recv.at[c],
-                device_id={"shard": q},
-                device_id_type=MESH,
-            ).start()
-
-        for j in range(cap):
-            arrived[c][me * cap + j] = updated[c, me, j]
-
     def unit(c, origin, h):
-        return pieces.at[c * nz + origin, pl.ds(h * half, half)]
+        return pieces.at[c * nz + origin, pl.ds(h * span, span)]
 
     def ring_copy(way, c, s, h):
         origin = lax.rem(z + (nz - s if way == 0 else s), nz)
@@ -267,28 +278,73 @@
             device_id_type=MESH,
         )
 
+    def send_own(c, h):
+        ring_copy(0, c, 0, h).start()
+        ring_copy(1, c, 0, h).start()
+
+    def goes(way, s, h):
+        return s < last or (s == last and h * 2 // UNITS == way)
+
+    whole_wait(came_g.at[pl.ds(0, (ns - 1) * cap)], swap_recv.at[0])
+    whole_wait(came_p.at[pl.ds(0, (ns - 1) * (cap - LATE))], swap_recv.at[1])
+    whole_wait(came_p.at[pl.ds(0, (ns - 1) * LATE)], swap_recv.at[2])
+    for h in range(UNITS):
+
+        @pl.loop(h * span, (h + 1) * span, unroll=UNROLL)
+        def _(b):
+            slot = slot_of[b]
+            factor = col_fac[me, pl.ds(jnp.clip(mats[b], 0, MATS - 1), 1), :]
+            pieces[z, b] = (came_p[slot].astype(f32) - came_g[slot] * factor).astype(jnp.bfloat16)
+
+        send_own(0, h)
+
+    @pl.loop(0, ns)
+    def _(q):
+        at = pl.ds(pl.multiple_of(q * LANES, LANES), LANES)
+        for j in range(cap):
+            factor = col_fac[q, pl.ds(matrix_of[j], 1), :]
+            value = p[j, :, at].astype(f32) - g[j, :, at] * row_fac[j] * factor
+            for c in range(1, CHUNKS):
+                updated[c - 1, q, j] = value[c * PART : (c + 1) * PART].astype(jnp.bfloat16)
+
+    for c in range(1, CHUNKS):
+
+        @pl.loop(1, ns)
+        def _(k):
+            q = lax.rem(me + k, ns)
+            pltpu.make_async_remote_copy(
+                updated.at[c - 1, q],
+                arrived[c].at[pl.ds(me * cap, cap)],
+                swap_send.at[c + 2],
+                swap_recv.at[c + 2],
+                device_id={"shard": q},
+                device_id_type=MESH,
+            ).start()
+
+        for j in range(cap):
+            arrived[c][me * cap + j] = updated[c - 1, me, j]
+
     def compact(c):
-        whole_wait(arrived[c].at[pl.ds(0, (ns - 1) * cap)], swap_recv.at[c])
-        for h in range(2):
-
-            @pl.loop(h * half, (h + 1) * half, unroll=8)
+        whole_wait(arrived[c].at[pl.ds(0, (ns - 1) * cap)], swap_recv.at[c + 2])
+        for h in range(UNITS):
+
+            @pl.loop(h * span, (h + 1) * span, unroll=UNROLL)
             def _(b):
                 pieces[c * nz + z, b] = arrived[c][slot_of[b]]
 
-            ring_copy(0, c, 0, h).start()
-            ring_copy(1, c, 0, h).start()
+            send_own(c, h)
 
     def take(c, s):
-        for h in range(2):
+        for h in range(UNITS):
             for way in range(2):
-                if s == last and h != way:
+                if not goes(way, s, h):
                     continue
                 origin = lax.rem(z + (nz - 1 - s if way == 0 else 1 + s), nz)
                 whole_wait(unit(c, origin, h), ring_recv.at[way, c, s, h])
-                if s + 1 < last or (s + 1 == last and h == way):
+                if s < last and goes(way, s + 1, h):
                     ring_copy(way, c, s + 1, h).start()
 
-    for c, s in sends(last):
+    for c, s in sends(last)[1:]:
         if s == 0:
             compact(c)
         else:
@@ -299,8 +355,11 @@
     whole_wait(from_plane.at[pl.ds(0, ns - 1)], small_send.at[0])
     whole_wait(from_line.at[pl.ds(0, nz - 1)], small_send.at[1])
     whole_wait(from_plane.at[pl.ds(0, ns - 1)], small_send.at[2])
-    for c in range(CHUNKS):
-        whole_wait(arrived[c].at[pl.ds(0, (ns - 1) * cap)], swap_send.at[c])
+    whole_wait(came_g.at[pl.ds(0, (ns - 1) * cap)], swap_send.at[0])
+    whole_wait(came_p.at[pl.ds(0, (ns - 1) * (cap - LATE))], swap_send.at[1])
+    whole_wait(came_p.at[pl.ds(0, (ns - 1) * LATE)], swap_send.at[2])
+    for c in range(1, CHUNKS):
+        whole_wait(arrived[c].at[pl.ds(0, (ns - 1) * cap)], swap_send.at[c + 2])
     for way in range(2):
         whole_wait(pieces.at[pl.ds(0, CHUNKS * last + CHUNKS // 2)], ring_send.at[way])
 
@@ -348,18 +407,22 @@
             pltpu.VMEM((cap, ROWS, LANES), f32),
             pltpu.VMEM((cap, ROWS, LANES), f32),
             pltpu.VMEM((ns, 8, LANES), f32),
-            pltpu.VMEM((CHUNKS, ns, cap, PART, LANES), bf16),
-            *[pltpu.VMEM((ns * cap, PART, LANES), bf16) for _ in range(CHUNKS)],
+            pltpu.VMEM((CHUNKS - 1, ns, cap, PART, LANES), bf16),
+            pltpu.VMEM((ns, cap, PART, LANES), f32),
+            pltpu.VMEM((ns, cap, PART, LANES), bf16),
+            pltpu.VMEM((ns * cap, PART, LANES), f32),
+            pltpu.VMEM((ns * cap, PART, LANES), bf16),
+            *[pltpu.VMEM((ns * cap, PART, LANES), bf16) for _ in range(CHUNKS - 1)],
             pltpu.SMEM((nb,), jnp.int32),
             pltpu.SMEM((cap * MATS,), f32),
             pltpu.SMEM((cap,), jnp.int32),
             dma((6,)),
             dma((3,)),
             dma((3,)),
-            dma((CHUNKS,)),
-            dma((CHUNKS,)),
+            dma((CHUNKS + 2,)),
+            dma((CHUNKS + 2,)),
             dma((2,)),
-            dma((2, CHUNKS, nz // 2, 2)),
+            dma((2, CHUNKS, nz // 2, UNITS)),
         ],
         compiler_params=pltpu.CompilerParams(collective_id=0, has_side_effects=True, vmem_limit_bytes=24 << 20),
         name="step",

time: 90.2 us -> 83.1 us (0.921)
  Pallas kernels: 87.3 us -> 80.6 us
    pallas_call x1, Pallas kernels: 84.8 us -> 78.1 us  [body(): pl.pallas_call(functools.partial(kernel, ns, nz, cap, nb), out_shape=(plt...]
where the time goes in v3:
time: 83.1 us; the launch traced here: 81.9 us
  Pallas kernels  80.6 us (97%)
  between operations  1.29 us (2%)
    pallas_call x1, Pallas kernels, body(): pl.pallas_call(functools.partial(kernel, ns, nz, cap, nb), out_shape=(plt...  78.1 us
    pallas_call x1, Pallas kernels, body(): pl.pallas_call(functools.partial(finish, nz), out_shape=(jax.ShapeDtypeSt...  2.48 us

profile of v3, /device:TPU:2, one launch (start us, length us, event | category | flops | bytes accessed | tf_op | source)
XLA Modules:
  0.0 81.9 jit_solution(11979873703654952934)
XLA Ops:
  1.3 78.1 %step.2 = (bf16[32,144,4,128]{3,2,1,0:T(4,128)(2,1)S(1)}, f32[9,16]{1,0:T(8,128)S(1)}, f32[3,4096]{1,0:T(4,128)S(1)}) custom-call(s32[1]{0:T(128)S(6)} %copy.10.step, s32[32]{0:T(128)} %starts_hbm.1, s32[144]{0:T(256)} %mats_hbm.1, f32[9,16,4096]{2,1,0:T(8,128)} %grad_hbm.1, bf16[9,16,4096]{2,1,0:T(8,128)(2,1)} %param_hbm.1, f32[9,16]{1,0:T(8,128)} %row_state_hbm.1, ...), custom_call_target="tpu_custom_call" | custom-call | tf_op jit(solution)/shard_map/step/pallas_call | solution.py:386
  79.4 2.5 %finish.1 = (bf16[144,8,4,4,128]{4,3,2,1,0:T(4,128)(2,1)}, f32[9,16]{1,0:T(8,128)}, f32[3,4096]{1,0:T(4,128)}) custom-call(bf16[32,144,4,128]{3,2,1,0:T(4,128)(2,1)S(1)} %get-tuple-element.9.pieces, f32[9,16]{1,0:T(8,128)S(1)} %get-tuple-element.10.rows, f32[3,4096]{1,0:T(4,128)S(1)} %get-tuple-element.11.cols), custom_call_target="tpu_custom_call" | custom-call | tf_op jit(solution)/shard_map/finish/pallas_call | solution.py:430

commit v4 on v3

--- a/solution.py
+++ b/solution.py
@@ -11,20 +11,37 @@
 LANES = 128
 ROWS = 16
 MATS = 3
-CHUNKS = 4
+PART = 2
+SIZES = (1, 1, 2, 4)
+FIRST = (0, 1, 2, 4)
+CHUNKS = len(SIZES)
 UNITS = 4
 UNROLL = 6
-LATE = 6
-PART = ROWS // CHUNKS
+UPDATE = -1
+ORDER = (
+    (1, UPDATE),
+    (0, 1),
+    (2, UPDATE),
+    (0, 2),
+    (1, 0),
+    (3, UPDATE),
+    (0, 3),
+    (1, 1),
+    (2, 0),
+    (1, 2),
+    (2, 1),
+    (1, 3),
+    (2, 2),
+    (3, 0),
+    (2, 3),
+    (3, 1),
+    (3, 2),
+    (3, 3),
+)
 
 
 def whole_wait(ref, sem):
     pltpu.make_async_copy(ref, ref, sem).wait()
-
-
-def sends(last):
-    order = [(c, s) for c in range(CHUNKS) for s in range(last + 1)]
-    return sorted(order, key=lambda at: (3.5 * at[0] + 2 * at[1] - 0.5 if at[0] else at[1] + max(0, at[1] - 2), at))
 
 
 def kernel(
@@ -39,7 +56,10 @@
     param_hbm,
     row_state_hbm,
     col_state_hbm,
-    pieces,
+    pieces_0,
+    pieces_1,
+    pieces_2,
+    pieces_3,
     out_rows,
     out_cols,
     starts,
@@ -56,7 +76,9 @@
     row_inv,
     row_fac,
     col_fac,
-    updated,
+    updated_1,
+    updated_2,
+    updated_3,
     early_g,
     early_p,
     came_g,
@@ -79,8 +101,14 @@
     z = lax.axis_index("dp")
     cols = ns * LANES
     f32 = jnp.float32
+
+    def peer(k):
+        return lax.rem(me + k, ns)
+
     span = nb // UNITS
     last = nz // 2 - 1
+    pieces = (pieces_0, pieces_1, pieces_2, pieces_3)
+    updated = (None, updated_1, updated_2, updated_3)
     arrived = (None, arrived_1, arrived_2, arrived_3)
 
     loads = [
@@ -96,13 +124,13 @@
             )
         )
     ]
-    for load in loads:
+    for load in loads[:5]:
         load.start()
     barrier = pltpu.get_barrier_semaphore()
 
     @pl.loop(1, ns)
     def _(k):
-        pl.semaphore_signal(barrier, inc=1, device_id={"shard": lax.rem(me + k, ns)}, device_id_type=MESH)
+        pl.semaphore_signal(barrier, inc=1, device_id={"shard": peer(k)}, device_id_type=MESH)
 
     @pl.loop(1, nz)
     def _(k):
@@ -127,6 +155,7 @@
     eye = sub == lane
 
     loads[3].wait()
+    loads[5].start()
     row_sums = [jnp.zeros((ROWS, 1), f32) for _ in range(MATS)]
     for j in range(cap):
         gj = g[j]
@@ -145,7 +174,7 @@
     for m in range(MATS):
         row_line = jnp.where(at_lane == m, jnp.sum(row_sums[m], axis=0, keepdims=True), row_line)
 
-    @pl.loop(0, ns)
+    @pl.loop(0, ns, unroll=4)
     def _(q):
         at = pl.ds(pl.multiple_of(q * LANES, LANES), LANES)
         acc = [jnp.zeros((8, LANES), f32) for _ in range(2 * MATS)]
@@ -170,7 +199,7 @@
 
     @pl.loop(1, ns)
     def _(k):
-        q = lax.rem(me + k, ns)
+        q = peer(k)
         pltpu.make_async_remote_copy(
             stat.at[q], from_plane.at[me], small_send.at[0], small_recv.at[0], device_id={"shard": q}, device_id_type=MESH
         ).start()
@@ -178,14 +207,11 @@
     loads[5].wait()
 
     def early(q):
-        now = cap - LATE
-        parts = ((early_g.at[q], me * cap, cap, came_g), (early_p.at[q, pl.ds(0, now)], me * cap, now, came_p))
-        parts += ((early_p.at[q, pl.ds(now, LATE)], me * cap + now, LATE, came_p),)
         return [
             pltpu.make_async_remote_copy(
-                source, target.at[pl.ds(at, size)], swap_send.at[i], swap_recv.at[i], device_id={"shard": q}, device_id_type=MESH
+                source.at[q], target.at[pl.ds(me * cap, cap)], swap_send.at[i], swap_recv.at[i], device_id={"shard": q}, device_id_type=MESH
             )
-            for i, (source, at, size, target) in enumerate(parts)
+            for i, (source, target) in enumerate(((early_g, came_g), (early_p, came_p)))
         ]
 
     def prepare(q, to_g, to_p, first_row):
@@ -200,8 +226,6 @@
     def _(k):
         q = lax.rem(me + k, ns)
         prepare(q, early_g.at[q], early_p.at[q], 0)
-        for copy in early(q)[:2]:
-            copy.start()
 
     def place(b, owner):
         following = starts[jnp.minimum(owner + 1, ns - 1)]
@@ -225,6 +249,11 @@
             mine.at[0], from_line.at[z], small_send.at[1], small_recv.at[1], device_id={"dp": other}, device_id_type=MESH
         ).start()
 
+    @pl.loop(1, ns)
+    def _(k):
+        for copy in early(peer(k)):
+            copy.start()
+
     whole_wait(from_line.at[pl.ds(0, nz - 1)], small_recv.at[1])
     both = from_line[0]
     for s in range(1, nz):
@@ -234,14 +263,10 @@
 
     @pl.loop(1, ns)
     def _(k):
-        q = lax.rem(me + k, ns)
+        q = peer(k)
         pltpu.make_async_remote_copy(
             mine.at[1], totals.at[me], small_send.at[2], small_recv.at[2], device_id={"shard": q}, device_id_type=MESH
         ).start()
-
-    @pl.loop(1, ns)
-    def _(k):
-        early(lax.rem(me + k, ns))[2].start()
 
     loads[4].wait()
     whole_wait(totals.at[pl.ds(0, ns - 1)], small_recv.at[2])
@@ -264,7 +289,7 @@
         col_fac[q, 0:MATS, :] = scale / jnp.sqrt(out_cols[:, pl.ds(q * LANES, LANES)])
 
     def unit(c, origin, h):
-        return pieces.at[c * nz + origin, pl.ds(h * span, span)]
+        return pieces[c].at[origin, pl.ds(h * span, span)]
 
     def ring_copy(way, c, s, h):
         origin = lax.rem(z + (nz - s if way == 0 else s), nz)
@@ -286,51 +311,57 @@
         return s < last or (s == last and h * 2 // UNITS == way)
 
     whole_wait(came_g.at[pl.ds(0, (ns - 1) * cap)], swap_recv.at[0])
-    whole_wait(came_p.at[pl.ds(0, (ns - 1) * (cap - LATE))], swap_recv.at[1])
-    whole_wait(came_p.at[pl.ds(0, (ns - 1) * LATE)], swap_recv.at[2])
+    whole_wait(came_p.at[pl.ds(0, (ns - 1) * cap)], swap_recv.at[1])
     for h in range(UNITS):
 
         @pl.loop(h * span, (h + 1) * span, unroll=UNROLL)
         def _(b):
             slot = slot_of[b]
             factor = col_fac[me, pl.ds(jnp.clip(mats[b], 0, MATS - 1), 1), :]
-            pieces[z, b] = (came_p[slot].astype(f32) - came_g[slot] * factor).astype(jnp.bfloat16)
+            pieces[0][z, b, 0] = (came_p[slot].astype(f32) - came_g[slot] * factor).astype(jnp.bfloat16)
 
         send_own(0, h)
 
-    @pl.loop(0, ns)
-    def _(q):
-        at = pl.ds(pl.multiple_of(q * LANES, LANES), LANES)
-        for j in range(cap):
-            factor = col_fac[q, pl.ds(matrix_of[j], 1), :]
-            value = p[j, :, at].astype(f32) - g[j, :, at] * row_fac[j] * factor
-            for c in range(1, CHUNKS):
-                updated[c - 1, q, j] = value[c * PART : (c + 1) * PART].astype(jnp.bfloat16)
-
-    for c in range(1, CHUNKS):
-
-        @pl.loop(1, ns)
+    def swap(c, q):
+        return pltpu.make_async_remote_copy(
+            updated[c].at[q],
+            arrived[c].at[pl.ds(me * cap, cap)],
+            swap_send.at[c + 1],
+            swap_recv.at[c + 1],
+            device_id={"shard": q},
+            device_id_type=MESH,
+        )
+
+    def update(c):
+        low = FIRST[c] * PART // 8 * 8
+        high = -(-(FIRST[c] + SIZES[c]) * PART // 8) * 8
+
+        @pl.loop(0, ns)
         def _(k):
             q = lax.rem(me + k, ns)
-            pltpu.make_async_remote_copy(
-                updated.at[c - 1, q],
-                arrived[c].at[pl.ds(me * cap, cap)],
-                swap_send.at[c + 2],
-                swap_recv.at[c + 2],
-                device_id={"shard": q},
-                device_id_type=MESH,
-            ).start()
-
+            at = pl.ds(pl.multiple_of(q * LANES, LANES), LANES)
+            for j in range(cap):
+                factor = col_fac[q, pl.ds(matrix_of[j], 1), :]
+                value = p[j, :, at].astype(f32)[low:high] - g[j, low:high, at] * row_fac[j, low:high] * factor
+                for i in range(SIZES[c]):
+                    top = (FIRST[c] + i) * PART - low
+                    updated[c][q, j, i] = value[top : top + PART].astype(jnp.bfloat16)
+
+            @pl.when(k > 1)
+            def _():
+                swap(c, lax.rem(me + k - 1, ns)).start()
+
+        swap(c, lax.rem(me + ns - 1, ns)).start()
         for j in range(cap):
-            arrived[c][me * cap + j] = updated[c - 1, me, j]
+            arrived[c][me * cap + j] = updated[c][me, j]
 
     def compact(c):
-        whole_wait(arrived[c].at[pl.ds(0, (ns - 1) * cap)], swap_recv.at[c + 2])
+        whole_wait(arrived[c].at[pl.ds(0, (ns - 1) * cap)], swap_recv.at[c + 1])
         for h in range(UNITS):
 
             @pl.loop(h * span, (h + 1) * span, unroll=UNROLL)
             def _(b):
-                pieces[c * nz + z, b] = arrived[c][slot_of[b]]
+                pieces[c][z, b] = arrived[c][slot_of[b]]
 
             send_own(c, h)
 
@@ -344,10 +375,12 @@
                 if s < last and goes(way, s + 1, h):
                     ring_copy(way, c, s + 1, h).start()
 
-    for c, s in sends(last)[1:]:
-        if s == 0:
+    for c, s in ORDER:
+        if s == UPDATE:
+            update(c)
+        elif s == 0:
             compact(c)
-        else:
+        elif s <= last:
             take(c, s - 1)
     for c in range(CHUNKS):
         take(c, last)
@@ -356,20 +389,18 @@
     whole_wait(from_line.at[pl.ds(0, nz - 1)], small_send.at[1])
     whole_wait(from_plane.at[pl.ds(0, ns - 1)], small_send.at[2])
     whole_wait(came_g.at[pl.ds(0, (ns - 1) * cap)], swap_send.at[0])
-    whole_wait(came_p.at[pl.ds(0, (ns - 1) * (cap - LATE))], swap_send.at[1])
-    whole_wait(came_p.at[pl.ds(0, (ns - 1) * LATE)], swap_send.at[2])
+    whole_wait(came_p.at[pl.ds(0, (ns - 1) * cap)], swap_send.at[1])
     for c in range(1, CHUNKS):
-        whole_wait(arrived[c].at[pl.ds(0, (ns - 1) * cap)], swap_send.at[c + 2])
+        whole_wait(arrived[c].at[pl.ds(0, (ns - 1) * cap)], swap_send.at[c + 1])
     for way in range(2):
-        whole_wait(pieces.at[pl.ds(0, CHUNKS * last + CHUNKS // 2)], ring_send.at[way])
-
-
-def finish(nz, pieces, rows, cols, out_params, out_rows, out_cols, sem):
-    copies = [
-        pltpu.make_async_copy(pieces.at[c * nz + s], out_params.at[:, s, c], sem.at[c * nz + s]) for c in range(CHUNKS) for s in range(nz)
-    ]
-    copies.append(pltpu.make_async_copy(rows, out_rows, sem.at[CHUNKS * nz]))
-    copies.append(pltpu.make_async_copy(cols, out_cols, sem.at[CHUNKS * nz + 1]))
+        whole_wait(pieces[-1].at[pl.ds(0, sum(SIZES) * (2 * last + 1) // (2 * SIZES[-1]))], ring_send.at[way])
+
+
+def finish(nz, *refs):
+    pieces, (rows, cols, out_params, out_rows, out_cols, sem) = refs[:CHUNKS], refs[CHUNKS:]
+    pairs = [(pieces[c].at[s], out_params.at[:, s, pl.ds(FIRST[c], SIZES[c])]) for c in range(CHUNKS) for s in range(nz)]
+    pairs += [(rows, out_rows), (cols, out_cols)]
+    copies = [pltpu.make_async_copy(source, target, sem.at[i]) for i, (source, target) in enumerate(pairs)]
     for copy in copies:
         copy.start()
     for copy in copies:
@@ -386,12 +417,12 @@
     landed = pl.pallas_call(
         functools.partial(kernel, ns, nz, cap, nb),
         out_shape=(
-            pltpu.VMEM((CHUNKS * nz, nb, PART, LANES), bf16),
+            *[pltpu.VMEM((nz, nb, size, PART, LANES), bf16) for size in SIZES],
             pltpu.VMEM(row_state.shape, f32),
             pltpu.VMEM(col_state.shape, f32),
         ),
         in_specs=[pl.BlockSpec(memory_space=pltpu.SMEM)] + [hbm] * 6,
-        out_specs=(vmem, vmem, vmem),
+        out_specs=(vmem,) * (CHUNKS + 2),
         scratch_shapes=[
             pltpu.SMEM(block_start.shape, jnp.int32),
             pltpu.SMEM(block_matrix.shape, jnp.int32),
@@ -407,20 +438,20 @@
             pltpu.VMEM((cap, ROWS, LANES), f32),
             pltpu.VMEM((cap, ROWS, LANES), f32),
             pltpu.VMEM((ns, 8, LANES), f32),
-            pltpu.VMEM((CHUNKS - 1, ns, cap, PART, LANES), bf16),
+            *[pltpu.VMEM((ns, cap, size, PART, LANES), bf16) for size in SIZES[1:]],
             pltpu.VMEM((ns, cap, PART, LANES), f32),
             pltpu.VMEM((ns, cap, PART, LANES), bf16),
             pltpu.VMEM((ns * cap, PART, LANES), f32),
             pltpu.VMEM((ns * cap, PART, LANES), bf16),
-            *[pltpu.VMEM((ns * cap, PART, LANES), bf16) for _ in range(CHUNKS - 1)],
+            *[pltpu.VMEM((ns * cap, size, PART, LANES), bf16) for size in SIZES[1:]],
             pltpu.SMEM((nb,), jnp.int32),
             pltpu.SMEM((cap * MATS,), f32),
             pltpu.SMEM((cap,), jnp.int32),
             dma((6,)),
             dma((3,)),
             dma((3,)),
-            dma((CHUNKS + 2,)),
-            dma((CHUNKS + 2,)),
+            dma((CHUNKS + 1,)),
+            dma((CHUNKS + 1,)),
             dma((2,)),
             dma((2, CHUNKS, nz // 2, UNITS)),
         ],
@@ -430,11 +461,11 @@
     new_params, new_rows, new_cols = pl.pallas_call(
         functools.partial(finish, nz),
         out_shape=(
-            jax.ShapeDtypeStruct((nb, nz, CHUNKS, PART, LANES), bf16),
+            jax.ShapeDtypeStruct((nb, nz, ROWS // PART, PART, LANES), bf16),
             jax.ShapeDtypeStruct(row_state.shape, f32),
             jax.ShapeDtypeStruct(col_state.shape, f32),
         ),
-        in_specs=[vmem] * 3,
+        in_specs=[vmem] * (CHUNKS + 2),
         out_specs=(hbm,) * 3,
         scratch_shapes=[dma((CHUNKS * nz + 2,))],
         compiler_params=pltpu.CompilerParams(vmem_limit_bytes=8 << 20),

time: 83.1 us -> 80.4 us (0.968); the launches traced: 81.9 us -> 80.1 us
  Pallas kernels: 80.6 us -> 78.8 us
    pallas_call x1, Pallas kernels: 78.1 us -> 76.4 us  [body(): pl.pallas_call(functools.partial(kernel, ns, nz, cap, nb), out_shape=(*[p...]
where the time goes in v4:
time: 80.4 us; the launch traced here: 80.1 us
  Pallas kernels  78.8 us (98%)
  between operations  1.29 us (2%)
    pallas_call x1, Pallas kernels, body(): pl.pallas_call(functools.partial(kernel, ns, nz, cap, nb), out_shape=(*[p...  76.4 us
    pallas_call x1, Pallas kernels, body(): pl.pallas_call(functools.partial(finish, nz), out_shape=(jax.ShapeDtypeSt...  2.48 us

profile of v4, /device:TPU:2, one launch (start us, length us, event | category | flops | bytes accessed | tf_op | source)
XLA Modules:
  0.0 80.1 jit_solution(14313007679775724722)
XLA Ops:
  1.3 76.4 %step.2 = (bf16[8,144,1,2,128]{4,3,2,1,0:T(2,128)(2,1)S(1)}, bf16[8,144,1,2,128]{4,3,2,1,0:T(2,128)(2,1)S(1)}, bf16[8,144,2,2,128]{4,3,2,1,0:T(2,128)(2,1)S(1)},...) custom-call(s32[1]{0:T(128)S(6)} %copy.10.step, s32[32]{0:T(128)} %starts_hbm.1, ...), custom_call_target="tpu_custom_call" | custom-call | tf_op jit(solution)/shard_map/step/pallas_call | solution.py:417
  77.6 2.5 %finish.1 = (bf16[144,8,8,2,128]{4,3,2,1,0:T(2,128)(2,1)}, f32[9,16]{1,0:T(8,128)}, f32[3,4096]{1,0:T(4,128)}) custom-call(bf16[8,144,1,2,128]{4,3,2,1,0:T(2,128)(2,1)S(1)} %get-tuple-element.12.refs_0_, bf16[8,144,1,2,128]{4,3,2,1,0:T(2,128)(2,1)S(1)} %get-tuple-element.13.refs_1_, bf16[8,144,2,2,128]{4,3,2,1,0:T(2,128)(2,1)S(1)} %get-tuple-element.14.refs_2_, ...), custom_call_target="tpu_custom_call" | custom-call | tf_op jit(solution)/shard_map/finish/pallas_call | solution.py:461

commit v5 on v4

--- a/solution.py
+++ b/solution.py
@@ -15,7 +15,7 @@
 SIZES = (1, 1, 2, 4)
 FIRST = (0, 1, 2, 4)
 CHUNKS = len(SIZES)
-UNITS = 4
+UNITS = (4, 2, 2, 4)
 UNROLL = 6
 UPDATE = -1
 ORDER = (
@@ -105,7 +105,7 @@
     def peer(k):
         return lax.rem(me + k, ns)
 
-    span = nb // UNITS
+    span = [nb // units for units in UNITS]
     last = nz // 2 - 1
     pieces = (pieces_0, pieces_1, pieces_2, pieces_3)
     updated = (None, updated_1, updated_2, updated_3)
@@ -289,7 +289,13 @@
         col_fac[q, 0:MATS, :] = scale / jnp.sqrt(out_cols[:, pl.ds(q * LANES, LANES)])
 
     def unit(c, origin, h):
-        return pieces[c].at[origin, pl.ds(h * span, span)]
+        return pieces[c].at[origin, pl.ds(h * span[c], span[c])]
+
+    def goes(way, c, s, h):
+        return s < last or (s == last and h * 2 // UNITS[c] == way)
+
+    hops = [(way, c, s, h) for c in range(CHUNKS) for s in range(last + 1) for h in range(UNITS[c]) for way in range(2)]
+    arrival = dict(zip((hop for hop in hops if goes(*hop)), range(len(hops)))).__getitem__
 
     def ring_copy(way, c, s, h):
         origin = lax.rem(z + (nz - s if way == 0 else s), nz)
@@ -298,7 +304,7 @@
             unit(c, origin, h),
             unit(c, origin, h),
             ring_send.at[way],
-            ring_recv.at[way, c, s, h],
+            ring_recv.at[arrival((way, c, s, h))],
             device_id={"dp": to},
             device_id_type=MESH,
         )
@@ -307,14 +313,11 @@
         ring_copy(0, c, 0, h).start()
         ring_copy(1, c, 0, h).start()
 
-    def goes(way, s, h):
-        return s < last or (s == last and h * 2 // UNITS == way)
-
     whole_wait(came_g.at[pl.ds(0, (ns - 1) * cap)], swap_recv.at[0])
     whole_wait(came_p.at[pl.ds(0, (ns - 1) * cap)], swap_recv.at[1])
-    for h in range(UNITS):
-
-        @pl.loop(h * span, (h + 1) * span, unroll=UNROLL)
+    for h in range(UNITS[0]):
+
+        @pl.loop(h * span[0], (h + 1) * span[0], unroll=UNROLL)
         def _(b):
             slot = slot_of[b]
             factor = col_fac[me, pl.ds(jnp.clip(mats[b], 0, MATS - 1), 1), :]
@@ -336,7 +339,7 @@
         low = FIRST[c] * PART // 8 * 8
         high = -(-(FIRST[c] + SIZES[c]) * PART // 8) * 8
 
-        @pl.loop(0, ns)
+        @pl.loop(0, ns, unroll=2)
         def _(k):
             q = lax.rem(me + k, ns)
             at = pl.ds(pl.multiple_of(q * LANES, LANES), LANES)
@@ -357,22 +360,22 @@
 
     def compact(c):
         whole_wait(arrived[c].at[pl.ds(0, (ns - 1) * cap)], swap_recv.at[c + 1])
-        for h in range(UNITS):
-
-            @pl.loop(h * span, (h + 1) * span, unroll=UNROLL)
+        for h in range(UNITS[c]):
+
+            @pl.loop(h * span[c], (h + 1) * span[c], unroll=UNROLL)
             def _(b):
                 pieces[c][z, b] = arrived[c][slot_of[b]]
 
             send_own(c, h)
 
     def take(c, s):
-        for h in range(UNITS):
+        for h in range(UNITS[c]):
             for way in range(2):
-                if not goes(way, s, h):
+                if not goes(way, c, s, h):
                     continue
                 origin = lax.rem(z + (nz - 1 - s if way == 0 else 1 + s), nz)
-                whole_wait(unit(c, origin, h), ring_recv.at[way, c, s, h])
-                if s < last and goes(way, s + 1, h):
+                whole_wait(unit(c, origin, h), ring_recv.at[arrival((way, c, s, h))])
+                if s < last and goes(way, c, s + 1, h):
                     ring_copy(way, c, s + 1, h).start()
 
     for c, s in ORDER:
@@ -398,13 +401,15 @@
 
 def finish(nz, *refs):
     pieces, (rows, cols, out_params, out_rows, out_cols, sem) = refs[:CHUNKS], refs[CHUNKS:]
-    pairs = [(pieces[c].at[s], out_params.at[:, s, pl.ds(FIRST[c], SIZES[c])]) for c in range(CHUNKS) for s in range(nz)]
-    pairs += [(rows, out_rows), (cols, out_cols)]
-    copies = [pltpu.make_async_copy(source, target, sem.at[i]) for i, (source, target) in enumerate(pairs)]
-    for copy in copies:
+    small = [pltpu.make_async_copy(rows, out_rows, sem.at[1]), pltpu.make_async_copy(cols, out_cols, sem.at[2])]
+    for copy in small:
         copy.start()
-    for copy in copies:
+    for c in range(CHUNKS):
+        for s in range(nz):
+            pltpu.make_async_copy(pieces[c].at[s], out_params.at[:, s, pl.ds(FIRST[c], SIZES[c])], sem.at[0]).start()
+    for copy in small:
         copy.wait()
+    whole_wait(out_params, sem.at[0])
 
 
 def body(ns, nz, grad, param, row_state, col_state, block_start, block_matrix, step):
@@ -453,7 +458,7 @@
             dma((CHUNKS + 1,)),
             dma((CHUNKS + 1,)),
             dma((2,)),
-            dma((2, CHUNKS, nz // 2, UNITS)),
+            dma((sum(UNITS) * (nz - 1),)),
         ],
         compiler_params=pltpu.CompilerParams(collective_id=0, has_side_effects=True, vmem_limit_bytes=24 << 20),
         name="step",
@@ -467,7 +472,7 @@
         ),
         in_specs=[vmem] * (CHUNKS + 2),
         out_specs=(hbm,) * 3,
-        scratch_shapes=[dma((CHUNKS * nz + 2,))],
+        scratch_shapes=[dma((3,))],
         compiler_params=pltpu.CompilerParams(vmem_limit_bytes=8 << 20),
         name="finish",
     )(*landed)

time: 80.4 us -> 79.9 us (level)
  no operation moved by 1% of the time
where the time goes in v5:
time: 79.9 us; the launch traced here: 79.7 us
  Pallas kernels  78.4 us (98%)
  between operations  1.29 us (2%)
    pallas_call x1, Pallas kernels, body(): pl.pallas_call(functools.partial(kernel, ns, nz, cap, nb), out_shape=(*[p...  76.2 us
    pallas_call x1, Pallas kernels, body(): pl.pallas_call(functools.partial(finish, nz), out_shape=(jax.ShapeDtypeSt...  2.21 us

profile of v5, /device:TPU:2, one launch (start us, length us, event | category | flops | bytes accessed | tf_op | source)
XLA Modules:
  0.0 79.7 jit_solution(12642026242361920070)
XLA Ops:
  1.3 76.2 %step.2 = (bf16[8,144,1,2,128]{4,3,2,1,0:T(2,128)(2,1)S(1)}, bf16[8,144,1,2,128]{4,3,2,1,0:T(2,128)(2,1)S(1)}, bf16[8,144,2,2,128]{4,3,2,1,0:T(2,128)(2,1)S(1)},...) custom-call(s32[1]{0:T(128)S(6)} %copy.10.step, s32[32]{0:T(128)} %starts_hbm.1, ...), custom_call_target="tpu_custom_call" | custom-call | tf_op jit(solution)/shard_map/step/pallas_call | solution.py:422
  77.5 2.2 %finish.1 = (bf16[144,8,8,2,128]{4,3,2,1,0:T(2,128)(2,1)}, f32[9,16]{1,0:T(8,128)}, f32[3,4096]{1,0:T(4,128)}) custom-call(bf16[8,144,1,2,128]{4,3,2,1,0:T(2,128)(2,1)S(1)} %get-tuple-element.12.refs_0_, bf16[8,144,1,2,128]{4,3,2,1,0:T(2,128)(2,1)S(1)} %get-tuple-element.13.refs_1_, bf16[8,144,2,2,128]{4,3,2,1,0:T(2,128)(2,1)S(1)} %get-tuple-element.14.refs_2_, ...), custom_call_target="tpu_custom_call" | custom-call | tf_op jit(solution)/shard_map/finish/pallas_call | solution.py:466

commit v6 on v5

--- a/solution.py
+++ b/solution.py
@@ -16,7 +16,7 @@
 FIRST = (0, 1, 2, 4)
 CHUNKS = len(SIZES)
 UNITS = (4, 2, 2, 4)
-UNROLL = 6
+UNROLL = 12
 UPDATE = -1
 ORDER = (
     (1, UPDATE),
@@ -174,7 +174,7 @@
     for m in range(MATS):
         row_line = jnp.where(at_lane == m, jnp.sum(row_sums[m], axis=0, keepdims=True), row_line)
 
-    @pl.loop(0, ns, unroll=4)
+    @pl.loop(0, ns, unroll=8)
     def _(q):
         at = pl.ds(pl.multiple_of(q * LANES, LANES), LANES)
         acc = [jnp.zeros((8, LANES), f32) for _ in range(2 * MATS)]

time: 79.9 us -> 79.9 us (level)
  no operation moved by 1% of the time
where the time goes in v6:
time: 79.9 us; the launch traced here: 79.6 us
  Pallas kernels  78.3 us (98%)
  between operations  1.29 us (2%)
    pallas_call x1, Pallas kernels, body(): pl.pallas_call(functools.partial(kernel, ns, nz, cap, nb), out_shape=(*[p...  76.1 us
    pallas_call x1, Pallas kernels, body(): pl.pallas_call(functools.partial(finish, nz), out_shape=(jax.ShapeDtypeSt...  2.21 us

profile of v6, /device:TPU:2, one launch (start us, length us, event | category | flops | bytes accessed | tf_op | source)
XLA Modules:
  0.0 79.6 jit_solution(7479119721927764224)
XLA Ops:
  1.3 76.1 %step.2 = (bf16[8,144,1,2,128]{4,3,2,1,0:T(2,128)(2,1)S(1)}, bf16[8,144,1,2,128]{4,3,2,1,0:T(2,128)(2,1)S(1)}, bf16[8,144,2,2,128]{4,3,2,1,0:T(2,128)(2,1)S(1)},...) custom-call(s32[1]{0:T(128)S(6)} %copy.10.step, s32[32]{0:T(128)} %starts_hbm.1, ...), custom_call_target="tpu_custom_call" | custom-call | tf_op jit(solution)/shard_map/step/pallas_call | solution.py:422
  77.4 2.2 %finish.1 = (bf16[144,8,8,2,128]{4,3,2,1,0:T(2,128)(2,1)}, f32[9,16]{1,0:T(8,128)}, f32[3,4096]{1,0:T(4,128)}) custom-call(bf16[8,144,1,2,128]{4,3,2,1,0:T(2,128)(2,1)S(1)} %get-tuple-element.12.refs_0_, bf16[8,144,1,2,128]{4,3,2,1,0:T(2,128)(2,1)S(1)} %get-tuple-element.13.refs_1_, bf16[8,144,2,2,128]{4,3,2,1,0:T(2,128)(2,1)S(1)} %get-tuple-element.14.refs_2_, ...), custom_call_target="tpu_custom_call" | custom-call | tf_op jit(solution)/shard_map/finish/pallas_call | solution.py:466
